TPU v7x, 32 devices: a whole 2x2x4 slice. The times are simulated.
32 devices in a mesh: batch: 2 (over x), w: 4 (over z), h: 4 (over y, core).
Axes of the slice: x: 2, y: 2, z: 4, core: 2. Of those that a mesh axis runs over, the one named last changes fastest.
Arguments:
- images: bfloat16 [32, 1024, 512, 4], P('batch', 'h', 'w'), parts along dimension 0
- down_w1: bfloat16 [3, 3, 4, 64], replicated
- down_b1: float32 [64], replicated
- refine_w1: bfloat16 [3, 3, 64, 64], replicated
- refine_b1: float32 [64], replicated
- down_w2: bfloat16 [3, 3, 64, 128], replicated
- down_b2: float32 [128], replicated
- refine_w2: bfloat16 [3, 3, 128, 128], replicated
- refine_b2: float32 [128], replicated
- down_w3: bfloat16 [3, 3, 128, 256], replicated
- down_b3: float32 [256], replicated
- refine_w3: bfloat16 [3, 3, 256, 256], replicated
- refine_b3: float32 [256], replicated
Outputs:
- output: bfloat16 [32, 128, 64, 256], P('batch', 'h', 'w'), parts along dimension 0
There are 2 independent parts. A program takes and returns all parts, laid end to end along the dimension named above; an argument that names none is the same for every part.
All inputs are finite; a program needn't handle non-finite values.
Results may differ from a plain program's by a relative error of at most 0.00333018.
Values are sent between devices in bfloat16 or wider.
A program may use at most 1 GiB of HBM per device.

v0:
```python
import functools

import jax
import jax.numpy as jnp
from jax import lax
from jax.experimental import pallas as pl
from jax.experimental.pallas import tpu as pltpu
from jax.sharding import PartitionSpec as P


DIM_NUMS = ('HWNC', 'HWIO', 'HWNC')

TOP, MID, BOT = 24, 256, 16
ROWS = TOP + MID + BOT
PAIRS = 75
STEPS = 3
STEP = 28
FIRST = -13
OUT_COLS = 14


def next_perm(axis_size):
    return [(src_dev, (src_dev + 1) % axis_size) for src_dev in range(axis_size)]


def prev_perm(axis_size):
    return [(src_dev, (src_dev - 1) % axis_size) for src_dev in range(axis_size)]


def lane_window(pieces, start, offset):
    lane = lax.broadcasted_iota(jnp.int32, pieces[0].shape, 1)
    total = None
    for chan, piece in enumerate(pieces):
        shift = (32 * chan + offset - start) % 128
        moved = pltpu.roll(piece, shift, 1) if shift else piece
        total = moved if total is None else jnp.where(lane >= 32 * chan, moved, total)
    return total


def blocked_loop(count, unroll, body):
    @pl.loop(0, count // unroll)
    def _(block):
        for part in range(unroll):
            body(unroll * block + part)

    for index in range(count - count % unroll, count):
        body(index)


def for_quads(sources, unroll, body):
    first = 0
    for source in sources:
        def one(quad, source=source, first=first):
            rows = [[source[4 * quad + row, chan] for chan in range(4)] for row in range(4)]
            body(first + quad, rows)

        blocked_loop(source.shape[0] // 4, unroll, one)
        first += source.shape[0] // 4


def pack_kernel(top_ref, mid_ref, bot_ref, to_next_ref, to_prev_ref):
    lane = lax.broadcasted_iota(jnp.int32, (16, 128), 1) % 32

    def body(quad, rows):
        last = [lane_window(rows[row], 115, 16 * (row % 2)) for row in range(4)]
        to_next_ref[2 * quad] = jnp.where(lane < 16, last[0], last[1])
        to_next_ref[2 * quad + 1] = jnp.where(lane < 16, last[2], last[3])
        packed = lane_window(rows[0], 0, 0)
        for row in range(1, 4):
            packed = jnp.where(lane >= 8 * row, lane_window(rows[row], 0, 8 * row), packed)
        to_prev_ref[quad] = packed

    for_quads((top_ref, mid_ref, bot_ref), 8, body)


def pack_halo(top, mid, bot):
    return pl.pallas_call(
        pack_kernel,
        out_shape=[
            jax.ShapeDtypeStruct((ROWS // 2, 16, 128), jnp.bfloat16),
            jax.ShapeDtypeStruct((ROWS // 4, 16, 128), jnp.bfloat16),
        ],
        cost_estimate=pl.CostEstimate(flops=8_000_000, bytes_accessed=6_000_000, transcendentals=0),
        name='pack',
    )(top, mid, bot)


def product(slab_ref, base, rows, windows, toep_ref, bias, store):
    lhs = []
    for row in range(rows):
        for win, _ in windows:
            taps = [slab_ref[base + 2 * row + tap, win] for tap in range(3)]
            lhs.append(jnp.concatenate(taps, axis=-1))
    lhs = jnp.concatenate(lhs, axis=0)
    most = max(count for _, count in windows)
    for chunk in range((most + 1) // 2):
        width = min(256, 128 * (most - 2 * chunk))
        acc = jnp.dot(lhs, toep_ref[:, 256 * chunk:256 * chunk + width], preferred_element_type=jnp.float32)
        acc = jnp.maximum(acc + bias[:, :width], 0.0).astype(jnp.bfloat16)
        acc = acc.reshape(rows, len(windows), 16, width)
        for index, (win, count) in enumerate(windows):
            for half in range(width // 128):
                pair = 2 * chunk + half
                if pair < count:
                    for row in range(rows):
                        store(row, win, pair, acc[row, index, :, 128 * half:128 * half + 128])


def main_kernel(top_ref, mid_ref, bot_ref, toep_ref, bias_ref, out_ref, own0_ref, own5_ref, slab_ref):
    step = pl.program_id(0)

    @pl.when(step == 0)
    def _():
        def body(quad, rows):
            for row in range(4):
                index = 4 * quad + row
                for win in range(4):
                    slab_ref[index, win] = lane_window(rows[row], FIRST + STEP * (win + 1), 0)
                own0_ref[index] = lane_window(rows[row], 0, 13)
                own5_ref[index] = lane_window(rows[row], 127, 0)

        for_quads((top_ref, mid_ref, bot_ref), 4, body)
        slab_ref[ROWS:ROWS + 8] = jnp.zeros((8, 4, 16, 128), jnp.bfloat16)

    bias = bias_ref[...]
    group = 5

    @pl.loop(0, PAIRS // STEPS // group)
    def _(part):
        first = group * part

        def store(row, win, pair, value):
            out_ref[first + row // 2, 7 * win + pair, :, 128 * (row % 2):128 * (row % 2) + 128] = value

        base = 4 * (PAIRS // STEPS * step + first) + 3
        product(slab_ref, base, 2 * group, [(win, 7) for win in range(4)], toep_ref, bias, store)


def whole(shape):
    return pl.BlockSpec(shape, lambda s: (0,) * len(shape), pipeline_mode=pl.Buffered(1))


def main_first(top, mid, bot, toep, bias):
    bf16 = jnp.bfloat16
    return pl.pallas_call(
        main_kernel,
        grid=(STEPS,),
        in_specs=[whole(x.shape) for x in (top, mid, bot, toep, bias)],
        out_specs=[
            pl.BlockSpec((PAIRS // STEPS, 28, 16, 256), lambda s: (s, 0, 0, 0)),
            whole((ROWS, 16, 128)),
            whole((ROWS, 16, 128)),
        ],
        out_shape=[
            jax.ShapeDtypeStruct((73, 28, 16, 256), bf16),
            jax.ShapeDtypeStruct((ROWS, 16, 128), bf16),
            jax.ShapeDtypeStruct((ROWS, 16, 128), bf16),
        ],
        scratch_shapes=[pltpu.VMEM((ROWS + 8, 4, 16, 128), bf16)],
        cost_estimate=pl.CostEstimate(flops=2 * 2400 * 4 * 512 * 1024, bytes_accessed=24_000_000, transcendentals=0),
        name='main_first',
    )(top, mid, bot, toep, bias)


def edge_kernel(own0_ref, own5_ref, from_prev_ref, from_next_ref, toep_ref, bias_ref, left_ref, right_ref, slab_ref):
    step = pl.program_id(0)

    @pl.when(step == 0)
    def _():
        lane = lax.broadcasted_iota(jnp.int32, (16, 128), 1) % 32

        def merge(quad):
            for row in range(4):
                index = 4 * quad + row
                left = from_prev_ref[2 * quad + row // 2]
                if row % 2:
                    left = pltpu.roll(left, 128 - 16, 1)
                slab_ref[index, 0] = jnp.where(lane < 13, left, own0_ref[index])
                right = pltpu.roll(from_next_ref[quad], (1 - 8 * row) % 128, 1)
                slab_ref[index, 1] = jnp.where(lane < 1, own5_ref[index], right)

        blocked_loop(ROWS // 4, 8, merge)
        slab_ref[ROWS:ROWS + 8] = jnp.zeros((8, 2, 16, 128), jnp.bfloat16)

    bias = bias_ref[...]
    base = 4 * (PAIRS // STEPS) * step + 3

    def store(row, win, pair, value):
        ref = right_ref if win else left_ref
        ref[row // 2, pair, :, 128 * (row % 2):128 * (row % 2) + 128] = value

    for window in ((0, 7), (1, 2)):
        product(slab_ref, base, 2 * (PAIRS // STEPS), [window], toep_ref, bias, store)


def edge_first(own0, own5, from_prev, from_next, toep, bias):
    bf16 = jnp.bfloat16
    args = (own0, own5, from_prev, from_next, toep, bias)
    return pl.pallas_call(
        edge_kernel,
        grid=(STEPS,),
        in_specs=[whole(x.shape) for x in args],
        out_specs=[
            pl.BlockSpec((PAIRS // STEPS, 7, 16, 256), lambda s: (s, 0, 0, 0)),
            pl.BlockSpec((PAIRS // STEPS, 2, 16, 256), lambda s: (s, 0, 0, 0)),
        ],
        out_shape=[
            jax.ShapeDtypeStruct((73, 7, 16, 256), bf16),
            jax.ShapeDtypeStruct((73, 2, 16, 256), bf16),
        ],
        scratch_shapes=[pltpu.VMEM((ROWS + 8, 2, 16, 128), bf16)],
        cost_estimate=pl.CostEstimate(flops=2 * 2400 * 512 * 1152, bytes_accessed=12_000_000, transcendentals=0),
        name='edge_first',
    )(*args)


def rows_kernel(taps, rows, group, parts, *refs):
    x_refs, (w_ref, bias_ref, out_ref) = refs[:parts], refs[parts:]
    cols = out_ref.shape[1]

    @pl.loop(0, rows // group)
    def _(part):
        first = group * part
        lhs = []
        for row in range(group):
            slabs = [slab.reshape(cols * 16, slab.shape[-1]) for slab in taps(x_refs, first + row)]
            lhs.append(jnp.concatenate(slabs, axis=-1))
        lhs = jnp.concatenate(lhs, axis=0)
        acc = jnp.dot(lhs, w_ref[...], preferred_element_type=jnp.float32)
        acc = jnp.maximum(acc + bias_ref[...], 0.0).astype(jnp.bfloat16)
        out_ref[pl.ds(first, group)] = acc.reshape(group, cols, 16, 256)


def rows_conv(xs, weight, bias, taps, halo, grid, rows, group, cols, out_rows, first_cols):
    def window(x, cut):
        start, size = cut
        block = (pl.Element(rows + halo), pl.Element(size)) + tuple(pl.Element(n) for n in x.shape[2:])
        rest = (0,) * (len(x.shape) - 2)
        return pl.BlockSpec(block, lambda s: (rows * s, start) + rest)

    out_shape = jax.ShapeDtypeStruct((out_rows, cols, 16, 256), jnp.bfloat16)
    flops = 2 * grid * rows * cols * 16 * weight.shape[0] * 256
    return pl.pallas_call(
        functools.partial(rows_kernel, taps, rows, group, len(xs)),
        grid=(grid,),
        in_specs=[window(x, cut) for x, cut in zip(xs, first_cols)] + [whole(weight.shape), whole((1, 256))],
        out_specs=pl.BlockSpec((rows, cols, 16, 256), lambda s: (s, 0, 0, 0)),
        out_shape=out_shape,
        cost_estimate=pl.CostEstimate(flops=flops, bytes_accessed=40_000_000, transcendentals=0),
    )(*xs, weight, bias.reshape(1, 256))


def refine1_taps(refs, row):
    left, main, right = refs
    slabs = []
    for tap in range(2):
        at = row + tap
        slabs.append(jnp.concatenate([left[at], main[at], right[at, 0:1]], axis=0))
        slabs.append(jnp.concatenate([left[at, 1:7], main[at], right[at]], axis=0))
    return slabs


def down2_taps(refs, row):
    (pairs,) = refs
    slabs = []
    for tap in range(2):
        lanes = 256 if tap == 0 else 128
        even, odd = pairs[row + tap, :, 0, :, :lanes], pairs[row + tap, :, 1, :, :lanes]
        slabs += [jnp.concatenate([odd[:1], odd[:-1]], axis=0), even, odd]
    return slabs


def refine2_taps(refs, row):
    (x,) = refs
    cols = x.shape[1] - 1
    return [x[row + tap, part:part + cols] for tap in range(3) for part in range(2)]


def pack_first(weight):
    cols = []
    for out_col in range(OUT_COLS):
        cols.append(jnp.pad(weight, ((0, 0), (2 * out_col, 29 - 2 * out_col), (0, 0), (0, 0))))
    stacked = jnp.concatenate(cols, axis=-1)
    return stacked.transpose(0, 2, 1, 3).reshape(384, 64 * OUT_COLS)


def pack_refine1(weight):
    wide = jnp.pad(weight, ((1, 1), (1, 1), (0, 0), (0, 0)))
    pieces = [wide[1 - r:5 - r, 1 - c:5 - c] for r in range(2) for c in range(2)]
    joined = jnp.concatenate(pieces, axis=-1)
    return joined.reshape(2, 2, 2, 2, 64, 256).transpose(0, 2, 1, 3, 4, 5).reshape(2, 2, 256, 256)


def pack_down2(weight):
    wide = jnp.pad(weight, ((0, 1), (2, 3), (0, 0), (0, 0)))
    joined = jnp.concatenate([wide[:, 2:8], wide[:, 0:6]], axis=-1)
    return joined.reshape(2, 2, 3, 2, 64, 256).transpose(0, 2, 1, 3, 4, 5).reshape(2, 3, 256, 256)


def pack_refine2(weight):
    wide = jnp.pad(weight, ((0, 0), (1, 1), (0, 0), (0, 0)))
    joined = jnp.concatenate([wide[:, 1:5], wide[:, 0:4]], axis=-1)
    return joined.reshape(3, 2, 256, 256)


def pack_down3(weight):
    return jnp.pad(weight, ((0, 0), (1, 0), (0, 0), (0, 0))).reshape(3, 2, 256, 256)


def conv(x, weight, bias, strides=(1, 1), pads=((0, 0), (0, 0))):
    out = lax.conv_general_dilated(x, weight, strides, pads, dimension_numbers=DIM_NUMS, preferred_element_type=jnp.float32)
    return lax.optimization_barrier(jnp.maximum(out + bias, 0.0).astype(jnp.bfloat16))


def solution(mesh):
    h_count = mesh.shape['h']
    w_count = mesh.shape['w']
    tile_spec = P('batch', 'h', 'w', None)

    def per_device(images, dw1, db1, rw1, rb1, dw2, db2, rw2, rb2, dw3, db3, rw3, rb3):
        native = images.transpose(0, 1, 3, 2)
        top = lax.ppermute(native[:, -TOP:], 'h', next_perm(h_count))
        bot = lax.ppermute(native[:, :BOT], 'h', prev_perm(h_count))
        top, mid, bot = (x.transpose(1, 2, 0, 3) for x in (top, native, bot))
        toep = pack_first(dw1)
        bias1 = jnp.tile(db1, 4).reshape(1, 256)
        to_next, to_prev = pack_halo(top, mid, bot)
        to_next, rw1, rb1, dw2, db2, rw2, rb2, dw3 = lax.optimization_barrier((to_next, rw1, rb1, dw2, db2, rw2, rb2, dw3))
        from_prev = lax.ppermute(to_next, 'w', next_perm(w_count))
        from_next = lax.ppermute(to_prev, 'w', prev_perm(w_count))
        y1_main, own0, own5 = main_first(top, mid, bot, toep, bias1)
        y1_left, y1_right = edge_first(own0, own5, from_prev, from_next, toep, bias1)
        rw1, dw2 = pack_refine1(rw1).reshape(1024, 256), pack_down2(dw2)
        dw2 = jnp.concatenate([dw2[0].reshape(768, 256), dw2[1, :, :128].reshape(384, 256)], axis=0)
        z1 = rows_conv((y1_left, y1_main, y1_right), rw1, jnp.tile(rb1, 4), refine1_taps, 1, 9, 8, 4, 36, 73, ((0, 7), (0, 28), (0, 2)))
        z1 = z1.reshape(73, 18, 2, 16, 256)
        y2 = rows_conv((z1,), dw2, jnp.tile(db2, 2), down2_taps, 1, 9, 8, 8, 18, 72, ((0, 18),))
        rw2, rb2, dw3 = pack_refine2(rw2), jnp.tile(rb2, 2), pack_down3(dw3)
        y2_edge = jnp.concatenate([y2[:, :3], y2[:, 15:18]], axis=2)
        z2_edge = conv(y2_edge, rw2, rb2)
        y3_edge = conv(z2_edge, dw3, db3, (2, 1))
        y3_left, y3_right = y3_edge[:, :, :16], y3_edge[:, :, 16:]
        from_left = lax.ppermute(y3_right, 'w', next_perm(w_count))
        from_right = lax.ppermute(y3_left, 'w', prev_perm(w_count))
        y2, y3_edge = lax.optimization_barrier((y2, y3_edge))
        z2_mid = rows_conv((y2,), rw2.reshape(1536, 256), rb2, refine2_taps, 2, 7, 10, 10, 13, 70, ((2, 14),))
        z2 = jnp.concatenate([z2_edge[:, 1:2, :16], z2_mid, z2_edge[:, 0:1, 16:]], axis=1)
        y3_mid = conv(z2, dw3, db3, (2, 1))
        y3_left, y3_right = y3_edge[:, :, :16], y3_edge[:, :, 16:]
        y3_left = jnp.concatenate([from_left, y3_left], axis=1)
        y3_right = jnp.concatenate([y3_right, from_right], axis=1)
        y3_left, y3_right = lax.optimization_barrier((y3_left, y3_right))
        y3 = jnp.concatenate([y3_left, y3_mid, y3_right], axis=1)
        z3 = conv(y3, rw3, rb3)
        return z3.transpose(2, 0, 1, 3)

    in_specs = (tile_spec,) + (P(),) * 12
    return jax.shard_map(per_device, mesh=mesh, in_specs=in_specs, out_specs=tile_spec, check_vma=False)
```

profile of v0, /device:TPU:0, one launch (start us, length us, event | category | flops | bytes accessed | tf_op | source)
XLA Modules:
  0.0 183.5 jit_solution(1074469433192942999)
XLA Ops:
  0.0 7.2 %copy.24 = bf16[16,256,128,4]{2,0,3,1:T(8,128)(2,1)S(1)} copy(bf16[16,256,128,4]{2,3,1,0:T(4,128)(2,1)} %param.13) | data formatting | bytes 8388608 | tf_op args[0]
  10.0 2.4 %collective-permute-start.1 = (bf16[16,16,4,128]{3,0,2,1:T(8,128)(2,1)}, bf16[16,16,4,128]{3,0,2,1:T(8,128)(2,1)S(1)}, u32[]{:S(2)}, u32[]{:S(2)}) collective-permute-start(bf16[16,16,4,128]{3,0,2,1:T(8,128)(2,1)} %slice.82), channel_id=1, source_target_pairs={{0,3},{1,0},{2,1},{3,2},{4,7},{5,4},{6,5},{7,6},{8,11},{9,8},{10,9... | collective-permute-start | bytes 786440 | tf_op jit(solution)/shard_map/ppermute | solution.py:323
  13.0 1.6 concatenate.30
  16.3 2.5 %collective-permute-done.1 = bf16[16,16,4,128]{3,0,2,1:T(8,128)(2,1)S(1)} collective-permute-done((bf16[16,16,4,128]{3,0,2,1:T(8,128)(2,1)}, bf16[16,16,4,128]{3,0,2,1:T(8,128)(2,1)S(1)}, u32[]{:S(2)}, u32[]{:S(2)}) %collective-permute-start.1) | collective-permute-done | bytes 262176 | tf_op jit(solution)/shard_map/ppermute | solution.py:323
  19.5 6.4 %pack.1 = (bf16[148,16,128]{2,1,0:T(8,128)(2,1)}, bf16[74,16,128]{2,1,0:T(8,128)(2,1)}) custom-call(bf16[24,4,16,128]{3,2,1,0:T(8,128)(2,1)} %bitcast.1.top_ref, bf16[256,4,16,128]{3,2,1,0:T(8,128)(2,1)} %bitcast.37, bf16[16,4,16,128]{3,2,1,0:T(8,128)(2,1)} %bitcast.54), custom_call_target="tpu_custom_call" | custom-call | flops 8000000 | bytes 6000000 | tf_op jit(solution)/shard_map/pack/pallas_call | solution.py:77
  25.9 1.6 collective-permute-start.2
  27.4 2.2 %collective-permute-start.3 = (bf16[74,16,128]{2,1,0:T(8,128)(2,1)}, bf16[74,16,128]{2,1,0:T(8,128)(2,1)}, u32[]{:S(2)}, u32[]{:S(2)}) collective-permute-start(bf16[74,16,128]{2,1,0:T(8,128)(2,1)} %get-tuple-element.28), channel_id=1, source_target_pairs={{0,12},{4,0},{8,4},{12,8},{1,13},{5,1},{9,5},{13,9},{2,14},{6,2},{... | collective-permute-start | bytes 909320 | tf_op jit(solution)/shard_map/ppermute | solution.py:330
  29.7 1.1 pad_slice_fusion.3
  31.0 1.2 pad_slice_fusion.7
  32.2 26.4 %main_first.1 = (bf16[73,28,16,256]{3,2,1,0:T(8,128)(2,1)}, bf16[296,16,128]{2,1,0:T(8,128)(2,1)}, bf16[296,16,128]{2,1,0:T(8,128)(2,1)}) custom-call(bf16[24,4,16,128]{3,2,1,0:T(8,128)(2,1)} %bitcast.1.top_ref, bf16[256,4,16,128]{3,2,1,0:T(8,128)(2,1)} %bitcast.38, bf16[16,4,16,128]{3,2,1,0:T(8,128)(2,1)} %bitcast.55, bf16[384,896]{1,0:T(8,128)(2,1)} %bitcast.51, ...), custom_call_target="tpu_custom_call" | custom-call | flops 10066329600 | bytes 24000000 | tf_op jit(solution)/shard_map/main_first/pallas_call | solution.py:145
  58.9 1.8 pad_maximum_fusion.5
  62.3 1.1 pad.89
  64.3 8.1 %edge_first.1 = (bf16[73,7,16,256]{3,2,1,0:T(8,128)(2,1)}, bf16[73,2,16,256]{3,2,1,0:T(8,128)(2,1)}) custom-call(bf16[296,16,128]{2,1,0:T(8,128)(2,1)} %get-tuple-element.24.own0_ref, bf16[296,16,128]{2,1,0:T(8,128)(2,1)} %get-tuple-element.25.own5_ref, bf16[148,16,128]{2,1,0:T(8,128)(2,1)} %collective-permute-done.2.from_prev_ref, ...), custom_call_target="tpu_custom_call" | custom-call | flops 2831155200 | bytes 12000000 | tf_op jit(solution)/shard_map/edge_first/pallas_call | solution.py:199
  72.4 29.5 %shard_map.127 = bf16[73,36,16,256]{3,2,1,0:T(8,128)(2,1)} custom-call(bf16[73,7,16,256]{3,2,1,0:T(8,128)(2,1)} %get-tuple-element.29.refs_0_, bf16[73,28,16,256]{3,2,1,0:T(8,128)(2,1)} %get-tuple-element.30.refs_1_, bf16[73,2,16,256]{3,2,1,0:T(8,128)(2,1)} %get-tuple-element.31.refs_2_, bf16[1024,256]{1,0:T(8,128)(2,1)} %bitcast.53, ...), custom_call_target="tpu_custom_call" | custom-call | flops 21743271936 | bytes 40000000 | tf_op jit(solution)/shard_map/pallas_call | solution.py:243
  102.5 20.3 %shard_map.128.refs_0_ = bf16[72,18,16,256]{3,2,1,0:T(8,128)(2,1)} custom-call(bf16[73,18,2,16,256]{4,3,2,1,0:T(8,128)(2,1)} %bitcast.56, bf16[1152,256]{1,0:T(8,128)(2,1)} %pad_maximum_fusion.2.refs_1_, f32[1,256]{1,0:T(1,128)} %bitcast.57), custom_call_target="tpu_custom_call" | custom-call | flops 12230590464 | bytes 40000000 | tf_op jit(solution)/shard_map/pallas_call | solution.py:243
  122.8 2.3 %fusion.27 = (bf16[72,3,16,256]{3,2,1,0:T(8,128)(2,1)S(1)}, bf16[72,3,16,256]{3,2,1,0:T(8,128)(2,1)S(1)}) fusion(bf16[72,18,16,256]{3,2,1,0:T(8,128)(2,1)} %shard_map.128.refs_0_), kind=kLoop, calls=%fused_computation.43 | loop fusion | bytes 7077888 | tf_op jit(solution)/shard_map/slice | solution.py:339
  125.0 4.0 %maximum_convert_fusion.2 = bf16[70,2,32,256]{3,2,1,0:T(8,128)(2,1)S(1)} fusion(f32[256]{0:T(256)S(1)} %broadcast_bitcast_fusion, bf16[3,2,256,256]{3,2,1,0:T(8,128)(2,1)S(1)} %bitcast.47, bf16[72,3,16,256]{3,2,1,0:T(8,128)(2,1)S(1)} %get-tuple-element.44, bf16[72,3,16,256]{3,2,1,0:T(8,128)(2,1)S(1)} %get-tuple-element.43), kind=kOutput, calls=%fused_computation.14 | convolution fusion | flops 3533733888 | bytes 6620160 | tf_op jit(solution)/shard_map/conv_general_dilated | solution.py:311
  130.0 1.0 fusion.23
  131.8 1.8 collective-permute-start.5
  134.2 15.5 %shard_map.129 = bf16[70,13,16,256]{3,2,1,0:T(8,128)(2,1)} custom-call(bf16[72,18,16,256]{3,2,1,0:T(8,128)(2,1)} %shard_map.128.refs_0_, bf16[1536,256]{1,0:T(8,128)(2,1)} %bitcast.48, f32[1,256]{1,0:T(1,128)} %bitcast.58), custom_call_target="tpu_custom_call" | custom-call | flops 11450449920 | bytes 40000000 | tf_op jit(solution)/shard_map/pallas_call | solution.py:243
  149.6 9.6 %maximum_convert_fusion.1 = bf16[34,14,16,256]{3,2,1,0:T(8,128)(2,1)S(1)} fusion(f32[256]{0:T(256)S(1)} %copy-done.9, bf16[3,2,256,256]{3,2,1,0:T(8,128)(2,1)S(1)} %bitcast.50, bf16[70,1,16,256]{3,2,1,0:T(8,128)(2,1)} %get-tuple-element.48, bf16[70,13,16,256]{3,2,1,0:T(8,128)(2,1)} %shard_map.129, bf16[70,1,16,256]{3,2,1,0:T(8,128)(2,1)S(1)} %get-tuple-element.47), kind=kOutput, calls=%fused_computation.7 | convolution fusion | flops 6003916800 | bytes 13288448 | tf_op jit(solution)/shard_map/conv_general_dilated | solution.py:311
  160.8 8.9 %collective-permute-done.4 = bf16[34,1,16,256]{3,2,1,0:T(8,128)(2,1)S(1)} collective-permute-done((bf16[34,1,16,256]{3,2,1,0:T(8,128)(2,1)S(1)}, bf16[34,1,16,256]{3,2,1,0:T(8,128)(2,1)S(1)}, u32[]{:S(2)}, u32[]{:S(2)}) %collective-permute-start.4) | collective-permute-done | bytes 278560 | tf_op jit(solution)/shard_map/ppermute | solution.py:343
  169.8 10.2 %maximum_convert_fusion = bf16[32,16,16,256]{3,2,1,0:T(8,128)(2,1)S(1)} fusion(f32[256]{0:T(256)S(1)} %copy-done.10, bf16[3,3,256,256]{3,2,1,0:T(8,128)(2,1)S(1)} %copy-done, bf16[34,2,16,256]{3,2,1,0:T(8,128)(2,1)S(1)} %pad_maximum_fusion.4, bf16[34,14,16,256]{3,2,1,0:T(8,128)(2,1)S(1)} %maximum_convert_fusion.1, ...), kind=kOutput, calls=%fused_computation.6 | convolution fusion | flops 9674981376 | bytes 10388480 | tf_op jit(solution)/shard_map/conv_general_dilated | solution.py:311
  180.0 3.5 %copy.19 = bf16[16,32,16,256]{3,2,1,0:T(8,128)(2,1)} copy(bf16[16,32,16,256]{3,0,2,1:T(8,128)(2,1)S(1)} %bitcast.39) | data formatting | bytes 8388608 | tf_op jit(solution)/shard_map/transpose | solution.py:355
  (57 shorter events, 13.0 us)
Async XLA Ops:
  0.0 169.8 %copy-start = (bf16[3,3,256,256]{3,2,1,0:T(8,128)(2,1)S(1)}, bf16[3,3,256,256]{3,2,1,0:T(8,128)(2,1)}, u32[]{:S(2)}) copy-start(bf16[3,3,256,256]{3,2,1,0:T(8,128)(2,1)} %param.24) | copy-start | bytes 3538948
  0.0 12.5 %copy-start.6 = (bf16[3,3,4,64]{3,2,1,0:T(4,128)(2,1)S(1)}, bf16[3,3,4,64]{3,2,1,0:T(4,128)(2,1)}, u32[]{:S(2)}) copy-start(bf16[3,3,4,64]{3,2,1,0:T(4,128)(2,1)} %param.14) | copy-start | bytes 13828
  7.2 2.1 %copy-start.1 = (bf16[16,256,128,4]{2,0,3,1:T(8,128)(2,1)}, bf16[16,256,128,4]{2,0,3,1:T(8,128)(2,1)S(1)}, u32[]{:S(2)}) copy-start(bf16[16,256,128,4]{2,0,3,1:T(8,128)(2,1)S(1)} %copy.24) | copy-start | bytes 12582916
  7.2 8.5 %copy-start.7 = (f32[64]{0:T(128)S(1)}, f32[64]{0:T(128)}, u32[]{:S(2)}) copy-start(f32[64]{0:T(128)} %param.15) | copy-start | bytes 772
  7.9 10.8 %collective-permute-start = (bf16[16,24,4,128]{3,0,2,1:T(8,128)(2,1)}, bf16[16,24,4,128]{3,0,2,1:T(8,128)(2,1)}, u32[]{:S(2)}, u32[]{:S(2)}) collective-permute-start(bf16[16,24,4,128]{3,0,2,1:T(8,128)(2,1)} %slice.81), channel_id=1, source_target_pairs={{0,1},{1,2},{2,3},{3,0},{4,5},{5,6},{6,7},{7,4},{8,9},{9,10},{10,1... | collective-permute-start | bytes 1179656 | tf_op jit(solution)/shard_map/ppermute | solution.py:322
  10.0 8.8 %collective-permute-start.1 = (bf16[16,16,4,128]{3,0,2,1:T(8,128)(2,1)}, bf16[16,16,4,128]{3,0,2,1:T(8,128)(2,1)S(1)}, u32[]{:S(2)}, u32[]{:S(2)}) collective-permute-start(bf16[16,16,4,128]{3,0,2,1:T(8,128)(2,1)} %slice.82), channel_id=1, source_target_pairs={{0,3},{1,0},{2,1},{3,2},{4,7},{5,4},{6,5},{7,6},{8,11},{9,8},{10,9... | collective-permute-start | bytes 786440 | tf_op jit(solution)/shard_map/ppermute | solution.py:323
  14.7 15.0 %copy-start.4 = (bf16[3,3,64,64]{3,2,1,0:T(8,128)(2,1)S(1)}, bf16[3,3,64,64]{3,2,1,0:T(8,128)(2,1)}, u32[]{:S(2)}) copy-start(bf16[3,3,64,64]{3,2,1,0:T(8,128)(2,1)} %param.16) | copy-start | bytes 221188
  14.7 16.2 %copy-start.5 = (bf16[3,3,64,128]{3,2,1,0:T(8,128)(2,1)S(1)}, bf16[3,3,64,128]{3,2,1,0:T(8,128)(2,1)}, u32[]{:S(2)}) copy-start(bf16[3,3,64,128]{3,2,1,0:T(8,128)(2,1)} %param.18) | copy-start | bytes 442372
  18.8 0.7 copy-start.3
  25.9 38.4 %collective-permute-start.2 = (bf16[148,16,128]{2,1,0:T(8,128)(2,1)}, bf16[148,16,128]{2,1,0:T(8,128)(2,1)}, u32[]{:S(2)}, u32[]{:S(2)}) collective-permute-start(bf16[148,16,128]{2,1,0:T(8,128)(2,1)} %get-tuple-element.27), channel_id=1, source_target_pairs={{0,4},{4,8},{8,12},{12,0},{1,5},{5,9},{9,13},{13,1},{2,6},{6,10},{... | collective-permute-start | bytes 1818632 | tf_op jit(solution)/shard_map/ppermute | solution.py:329
  27.4 36.8 %collective-permute-start.3 = (bf16[74,16,128]{2,1,0:T(8,128)(2,1)}, bf16[74,16,128]{2,1,0:T(8,128)(2,1)}, u32[]{:S(2)}, u32[]{:S(2)}) collective-permute-start(bf16[74,16,128]{2,1,0:T(8,128)(2,1)} %get-tuple-element.28), channel_id=1, source_target_pairs={{0,12},{4,0},{8,4},{12,8},{1,13},{5,1},{9,5},{13,9},{2,14},{6,2},{... | collective-permute-start | bytes 909320 | tf_op jit(solution)/shard_map/ppermute | solution.py:330
  32.2 26.6 %copy-start.12 = (f32[128]{0:T(128)S(1)}, f32[128]{0:T(128)}, u32[]{:S(2)}) copy-start(f32[128]{0:T(128)} %param.21) | copy-start | bytes 1540
  58.6 2.9 %copy-start.8 = (f32[64]{0:T(128)S(1)}, f32[64]{0:T(128)}, u32[]{:S(2)}) copy-start(f32[64]{0:T(128)} %param.17) | copy-start | bytes 772
  58.8 66.2 %copy-start.2 = (bf16[3,4,128,256]{3,2,1,0:T(8,128)(2,1)}, bf16[3,4,128,256]{3,2,1,0:T(8,128)(2,1)S(1)}, u32[]{:S(2)}) copy-start(bf16[3,4,128,256]{3,2,1,0:T(8,128)(2,1)S(1)} %pad_maximum_fusion.1) | copy-start | bytes 2359300
  72.4 29.5 %copy-start.11 = (f32[128]{0:T(128)S(1)}, f32[128]{0:T(128)}, u32[]{:S(2)}) copy-start(f32[128]{0:T(128)} %param.19) | copy-start | bytes 1540
  125.0 5.0 %copy-start.9 = (f32[256]{0:T(256)S(1)}, f32[256]{0:T(256)}, u32[]{:S(2)}) copy-start(f32[256]{0:T(256)} %param.23) | copy-start | bytes 3076
  131.8 28.0 %collective-permute-start.5 = (bf16[34,1,16,256]{3,2,1,0:T(8,128)(2,1)}, bf16[34,1,16,256]{3,2,1,0:T(8,128)(2,1)}, u32[]{:S(2)}, u32[]{:S(2)}) collective-permute-start(bf16[34,1,16,256]{3,2,1,0:T(8,128)(2,1)} %get-tuple-element.53), channel_id=1, source_target_pairs={{0,12},{4,0},{8,4},{12,8},{1,13},{5,1},{9,5},{13,9},{2,14},{6,2},{... | collective-permute-start | bytes 835592 | tf_op jit(solution)/shard_map/ppermute | solution.py:344
  149.6 20.2 %copy-start.10 = (f32[256]{0:T(256)S(1)}, f32[256]{0:T(256)}, u32[]{:S(2)}) copy-start(f32[256]{0:T(256)} %param.25) | copy-start | bytes 3076
  159.2 10.5 %collective-permute-start.4 = (bf16[34,1,16,256]{3,2,1,0:T(8,128)(2,1)S(1)}, bf16[34,1,16,256]{3,2,1,0:T(8,128)(2,1)S(1)}, u32[]{:S(2)}, u32[]{:S(2)}) collective-permute-start(bf16[34,1,16,256]{3,2,1,0:T(8,128)(2,1)S(1)} %get-tuple-element.54), channel_id=1, source_target_pairs={{0,4},{4,8},{8,12},{12,0},{1,5},{5,9},{9,13},{13,1},{2,6},{6,10},{... | collective-permute-start | bytes 835592 | tf_op jit(solution)/shard_map/ppermute | solution.py:343
where the time goes:
time: 184 us
  Pallas kernels  106 us (58%)
  local copies, waits for them, and re-layouts  27.9 us (15%)
  matrix products  24.9 us (14%)
  waiting for transfers between devices  11.4 us (6%)
  starting transfers between devices  9.08 us (5%)
  other arithmetic  3.94 us (2%)
    pallas_call x3, Pallas kernels, rows_conv(): pl.pallas_call(functools.partial(rows_kernel, taps, rows, group, len(xs))...  65.3 us
    pallas_call x1, Pallas kernels, main_first(): pl.pallas_call(main_kernel, grid=(STEPS,), in_specs=[whole(x.shape) for x...  26.4 us
    conv_general_dilated x4, matrix products, conv(): lax.conv_general_dilated(x, weight, strides, pads, dimension_numbers=DIM_...  24.9 us
    ppermute x1, waiting for transfers between devices, per_device(): from_left = lax.ppermute(y3_right, 'w', next_perm(w_count))  8.91 us
    unnamed x27, local copies, waits for them, and re-layouts  8.78 us
    pallas_call x1, Pallas kernels, edge_first(): pl.pallas_call(edge_kernel, grid=(STEPS,), in_specs=[whole(x.shape) for x...  8.08 us
    pallas_call x1, Pallas kernels, pack_halo(): pl.pallas_call(pack_kernel, out_shape=[jax.ShapeDtypeStruct((ROWS // 2, 1...  6.35 us
  transfers between devices with their start and end apart: 6, of which 2 were waited for; matrix products, arithmetic and copies ran while one was open for 13% of the time, Pallas kernels for 23%

commit v1 on v0

--- a/solution.py
+++ b/solution.py
@@ -247,7 +247,7 @@
         out_specs=pl.BlockSpec((rows, cols, 16, 256), lambda s: (s, 0, 0, 0)),
         out_shape=out_shape,
         cost_estimate=pl.CostEstimate(flops=flops, bytes_accessed=40_000_000, transcendentals=0),
-    )(*xs, weight, bias.reshape(1, 256))
+    )(*xs, weight, bias)
 
 
 def refine1_taps(refs, row):
@@ -270,12 +270,6 @@
     return slabs
 
 
-def refine2_taps(refs, row):
-    (x,) = refs
-    cols = x.shape[1] - 1
-    return [x[row + tap, part:part + cols] for tap in range(3) for part in range(2)]
-
-
 def pack_first(weight):
     cols = []
     for out_col in range(OUT_COLS):
@@ -284,27 +278,46 @@
     return stacked.transpose(0, 2, 1, 3).reshape(384, 64 * OUT_COLS)
 
 
-def pack_refine1(weight):
-    wide = jnp.pad(weight, ((1, 1), (1, 1), (0, 0), (0, 0)))
-    pieces = [wide[1 - r:5 - r, 1 - c:5 - c] for r in range(2) for c in range(2)]
-    joined = jnp.concatenate(pieces, axis=-1)
-    return joined.reshape(2, 2, 2, 2, 64, 256).transpose(0, 2, 1, 3, 4, 5).reshape(2, 2, 256, 256)
-
-
-def pack_down2(weight):
-    wide = jnp.pad(weight, ((0, 1), (2, 3), (0, 0), (0, 0)))
-    joined = jnp.concatenate([wide[:, 2:8], wide[:, 0:6]], axis=-1)
-    return joined.reshape(2, 2, 3, 2, 64, 256).transpose(0, 2, 1, 3, 4, 5).reshape(2, 3, 256, 256)
-
-
-def pack_refine2(weight):
-    wide = jnp.pad(weight, ((0, 0), (1, 1), (0, 0), (0, 0)))
-    joined = jnp.concatenate([wide[:, 1:5], wide[:, 0:4]], axis=-1)
-    return joined.reshape(3, 2, 256, 256)
-
-
-def pack_down3(weight):
-    return jnp.pad(weight, ((0, 0), (1, 0), (0, 0), (0, 0))).reshape(3, 2, 256, 256)
+def weights_kernel(rw1_ref, rb1_ref, dw2_ref, db2_ref, rw2_ref, rb2_ref, dw3_ref, rw1_out, rb1_out, dw2_out, db2_out, rw2_out, rb2_out, dw3_out):
+    def tap(ref, a, b):
+        if 0 <= a <= 2 and 0 <= b <= 2:
+            return ref[a, b]
+        return jnp.zeros(ref.shape[2:], ref.dtype)
+
+    for big_a in range(2):
+        for big_b in range(2):
+            for r in range(2):
+                for c in range(2):
+                    row = 64 * (8 * big_a + 4 * big_b + 2 * r + c)
+                    pieces = [tap(rw1_ref, 2 * big_a + r - r_out, 2 * big_b + c - c_out) for r_out in range(2) for c_out in range(2)]
+                    rw1_out[row:row + 64] = jnp.concatenate(pieces, axis=-1)
+    row = 0
+    for big_a in range(2):
+        for big_b in range(3):
+            for r in range(2 - big_a):
+                for c in range(2):
+                    pieces = [tap(dw2_ref, 2 * big_a + r, 2 * big_b + c - 2 * c_out) for c_out in range(2)]
+                    dw2_out[row:row + 64] = jnp.concatenate(pieces, axis=-1)
+                    row += 64
+    for a in range(3):
+        for b in range(4):
+            row = 128 * (4 * a + b)
+            pieces = [tap(rw2_ref, a, b - c_out) for c_out in range(2)]
+            rw2_out[row:row + 128] = jnp.concatenate(pieces, axis=-1)
+            dw3_out[row:row + 128] = tap(dw3_ref, a, b - 1)
+    rb1_out[...] = jnp.concatenate([rb1_ref[...]] * 4, axis=-1)
+    db2_out[...] = jnp.concatenate([db2_ref[...]] * 2, axis=-1)
+    rb2_out[...] = jnp.concatenate([rb2_ref[...]] * 2, axis=-1)
+
+
+def pack_weights(rw1, rb1, dw2, db2, rw2, rb2, dw3):
+    rows = (1024, 1, 1152, 1, 1536, 1, 1536)
+    return pl.pallas_call(
+        weights_kernel,
+        out_shape=[jax.ShapeDtypeStruct((n, 256), jnp.float32 if n == 1 else jnp.bfloat16) for n in rows],
+        cost_estimate=pl.CostEstimate(flops=4_000_000, bytes_accessed=5_000_000, transcendentals=0),
+        name='weights',
+    )(rw1, rb1.reshape(1, 64), dw2, db2.reshape(1, 128), rw2, rb2.reshape(1, 128), dw3)
 
 
 def conv(x, weight, bias, strides=(1, 1), pads=((0, 0), (0, 0))):
@@ -330,12 +343,11 @@
         from_next = lax.ppermute(to_prev, 'w', prev_perm(w_count))
         y1_main, own0, own5 = main_first(top, mid, bot, toep, bias1)
         y1_left, y1_right = edge_first(own0, own5, from_prev, from_next, toep, bias1)
-        rw1, dw2 = pack_refine1(rw1).reshape(1024, 256), pack_down2(dw2)
-        dw2 = jnp.concatenate([dw2[0].reshape(768, 256), dw2[1, :, :128].reshape(384, 256)], axis=0)
-        z1 = rows_conv((y1_left, y1_main, y1_right), rw1, jnp.tile(rb1, 4), refine1_taps, 1, 9, 8, 4, 36, 73, ((0, 7), (0, 28), (0, 2)))
+        rw1, rb1, dw2, db2, rw2, rb2, dw3 = pack_weights(rw1, rb1, dw2, db2, rw2, rb2, dw3)
+        rw2, dw3 = rw2.reshape(3, 2, 256, 256), dw3.reshape(3, 2, 256, 256)
+        z1 = rows_conv((y1_left, y1_main, y1_right), rw1, rb1, refine1_taps, 1, 9, 8, 4, 36, 73, ((0, 7), (0, 28), (0, 2)))
         z1 = z1.reshape(73, 18, 2, 16, 256)
-        y2 = rows_conv((z1,), dw2, jnp.tile(db2, 2), down2_taps, 1, 9, 8, 8, 18, 72, ((0, 18),))
-        rw2, rb2, dw3 = pack_refine2(rw2), jnp.tile(rb2, 2), pack_down3(dw3)
+        y2 = rows_conv((z1,), dw2, db2, down2_taps, 1, 9, 8, 8, 18, 72, ((0, 18),))
         y2_edge = jnp.concatenate([y2[:, :3], y2[:, 15:18]], axis=2)
         z2_edge = conv(y2_edge, rw2, rb2)
         y3_edge = conv(z2_edge, dw3, db3, (2, 1))
@@ -343,7 +355,7 @@
         from_left = lax.ppermute(y3_right, 'w', next_perm(w_count))
         from_right = lax.ppermute(y3_left, 'w', prev_perm(w_count))
         y2, y3_edge = lax.optimization_barrier((y2, y3_edge))
-        z2_mid = rows_conv((y2,), rw2.reshape(1536, 256), rb2, refine2_taps, 2, 7, 10, 10, 13, 70, ((2, 14),))
+        z2_mid = conv(y2[:, 2:16], rw2, rb2)
         z2 = jnp.concatenate([z2_edge[:, 1:2, :16], z2_mid, z2_edge[:, 0:1, 16:]], axis=1)
         y3_mid = conv(z2, dw3, db3, (2, 1))
         y3_left, y3_right = y3_edge[:, :, :16], y3_edge[:, :, 16:]

time: 184 us -> 164 us (0.89)
  Pallas kernels: 106 us -> 93.5 us
  matrix products: 24.9 us -> 35.4 us
  waiting for transfers between devices: 11.4 us -> 2.62 us
  local copies, waits for them, and re-layouts: 27.9 us -> 21 us
  other arithmetic: 3.94 us -> 0.13 us
    pallas_call x3 -> x2, Pallas kernels: 65.3 us -> 49.8 us  [rows_conv(): pl.pallas_call(functools.partial(rows_kernel, taps, rows, group, len(xs))...]
    conv_general_dilated x4 -> x5, matrix products: 24.9 us -> 35.4 us  [conv(): lax.conv_general_dilated(x, weight, strides, pads, dimension_numbers=DIM_...]
    ppermute x1, waiting for transfers between devices: 8.91 us -> 0.01 us  [per_device(): from_left = lax.ppermute(y3_right, 'w', next_perm(w_count))]
    pallas_call x0 -> x1, Pallas kernels: none -> 3 us  [pack_weights(): pl.pallas_call(weights_kernel, out_shape=[jax.ShapeDtypeStruct((n, 256),...]
    concatenate x4 -> x0, other arithmetic: 2.87 us -> none  [the longest x1 1.83 us: pack_refine1(): joined = jnp.concatenate(pieces, axis=-1)]
    slice x5 -> x0, local copies, waits for them, and re-layouts: 2.51 us -> none  [the longest x1 1.17 us: pack_refine2(): joined = jnp.concatenate([wide[:, 1:5], wide[:, 0:4]], axis=-1)]
    ppermute x1, starting transfers between devices: 1.8 us -> 3.88 us  [per_device(): from_right = lax.ppermute(y3_left, 'w', prev_perm(w_count))]
    unnamed x27 -> x31, local copies, waits for them, and re-layouts: 8.78 us -> 9.55 us
  transfers between devices with their start and end apart: 6 -> 6, of which waited for: 2 -> 1; matrix products, arithmetic and copies ran while one was open for 13% -> 15% of each run, Pallas kernels for 23% -> 18%
where the time goes in v1:
time: 164 us; the launch traced here: 163 us
  Pallas kernels  93.5 us (57%)
  matrix products  35.4 us (22%)
  local copies, waits for them, and re-layouts  21 us (13%)
  starting transfers between devices  10.4 us (6%)
  waiting for transfers between devices  2.62 us (2%)
    pallas_call x2, Pallas kernels, rows_conv(): pl.pallas_call(functools.partial(rows_kernel, taps, rows, group, len(xs))...  49.8 us
    conv_general_dilated x5, matrix products, conv(): lax.conv_general_dilated(x, weight, strides, pads, dimension_numbers=DIM_...  35.4 us
    pallas_call x1, Pallas kernels, main_first(): pl.pallas_call(main_kernel, grid=(STEPS,), in_specs=[whole(x.shape) for x...  26.3 us
    unnamed x31, local copies, waits for them, and re-layouts  9.55 us
    pallas_call x1, Pallas kernels, edge_first(): pl.pallas_call(edge_kernel, grid=(STEPS,), in_specs=[whole(x.shape) for x...  8.05 us
    pallas_call x1, Pallas kernels, pack_halo(): pl.pallas_call(pack_kernel, out_shape=[jax.ShapeDtypeStruct((ROWS // 2, 1...  6.35 us
    ppermute x1, starting transfers between devices, per_device(): from_right = lax.ppermute(y3_left, 'w', prev_perm(w_count))  3.88 us
    ppermute x1, starting transfers between devices, per_device(): from_next = lax.ppermute(to_prev, 'w', prev_perm(w_count))  3.6 us
  transfers between devices with their start and end apart: 6, of which 1 were waited for; matrix products, arithmetic and copies ran while one was open for 15% of the time, Pallas kernels for 18%

profile of v1, /device:TPU:0, one launch (start us, length us, event | category | flops | bytes accessed | tf_op | source)
XLA Modules:
  0.0 163.4 jit_solution(9414707992467209556)
XLA Ops:
  0.0 7.1 %copy.20 = bf16[16,256,128,4]{2,0,3,1:T(8,128)(2,1)S(1)} copy(bf16[16,256,128,4]{2,3,1,0:T(4,128)(2,1)} %param.13) | data formatting | bytes 8388608 | tf_op args[0]
  7.2 0.9 slice.41
  8.5 0.8 copy-done.1
  9.3 0.7 slice.42
  10.0 2.4 %collective-permute-start.1 = (bf16[16,16,4,128]{3,0,2,1:T(8,128)(2,1)}, bf16[16,16,4,128]{3,0,2,1:T(8,128)(2,1)S(1)}, u32[]{:S(2)}, u32[]{:S(2)}) collective-permute-start(bf16[16,16,4,128]{3,0,2,1:T(8,128)(2,1)} %slice.42), channel_id=1, source_target_pairs={{0,3},{1,0},{2,1},{3,2},{4,7},{5,4},{6,5},{7,6},{8,11},{9,8},{10,9... | collective-permute-start | bytes 786440 | tf_op jit(solution)/shard_map/ppermute | solution.py:336
  13.7 1.6 %concatenate.18 = bf16[3,32,4,896]{3,2,1,0:T(4,128)(2,1)S(1)} concatenate(bf16[3,32,4,64]{3,2,1,0:T(4,128)(2,1)S(1)} %get-tuple-element.80, bf16[3,32,4,64]{3,2,1,0:T(4,128)(2,1)S(1)} %get-tuple-element.79, bf16[3,32,4,64]{3,2,1,0:T(4,128)(2,1)S(1)} %get-tuple-element.78, bf16[3,32,4,64]{3,2,1,0:T(4,128)(2,1)S(1)} %get-tuple-element.77, ...), dimensions={3} | concatenate | bytes 1376256 | tf_op jit(solution)/shard_map/concatenate | solution.py:277
  15.3 0.9 copy.16
  16.3 2.6 %collective-permute-done.1 = bf16[16,16,4,128]{3,0,2,1:T(8,128)(2,1)S(1)} collective-permute-done((bf16[16,16,4,128]{3,0,2,1:T(8,128)(2,1)}, bf16[16,16,4,128]{3,0,2,1:T(8,128)(2,1)S(1)}, u32[]{:S(2)}, u32[]{:S(2)}) %collective-permute-start.1) | collective-permute-done | bytes 262176 | tf_op jit(solution)/shard_map/ppermute | solution.py:336
  19.5 6.3 %pack.1 = (bf16[148,16,128]{2,1,0:T(8,128)(2,1)}, bf16[74,16,128]{2,1,0:T(8,128)(2,1)}) custom-call(bf16[24,4,16,128]{3,2,1,0:T(8,128)(2,1)} %bitcast.1.top_ref, bf16[256,4,16,128]{3,2,1,0:T(8,128)(2,1)} %bitcast.26, bf16[16,4,16,128]{3,2,1,0:T(8,128)(2,1)} %bitcast.34), custom_call_target="tpu_custom_call" | custom-call | flops 8000000 | bytes 6000000 | tf_op jit(solution)/shard_map/pack/pallas_call | solution.py:77
  25.9 3.6 %collective-permute-start.3 = (bf16[74,16,128]{2,1,0:T(8,128)(2,1)}, bf16[74,16,128]{2,1,0:T(8,128)(2,1)S(1)}, u32[]{:S(2)}, u32[]{:S(2)}) collective-permute-start(bf16[74,16,128]{2,1,0:T(8,128)(2,1)} %get-tuple-element.35), channel_id=1, source_target_pairs={{0,12},{4,0},{8,4},{12,8},{1,13},{5,1},{9,5},{13,9},{2,14},{6,2},{... | collective-permute-start | bytes 909320 | tf_op jit(solution)/shard_map/ppermute | solution.py:343
  29.5 26.3 %main_first.1 = (bf16[73,28,16,256]{3,2,1,0:T(8,128)(2,1)}, bf16[296,16,128]{2,1,0:T(8,128)(2,1)}, bf16[296,16,128]{2,1,0:T(8,128)(2,1)}) custom-call(bf16[24,4,16,128]{3,2,1,0:T(8,128)(2,1)} %bitcast.1.top_ref, bf16[256,4,16,128]{3,2,1,0:T(8,128)(2,1)} %bitcast.27, bf16[16,4,16,128]{3,2,1,0:T(8,128)(2,1)} %bitcast.35, bf16[384,896]{1,0:T(8,128)(2,1)} %bitcast.32, ...), custom_call_target="tpu_custom_call" | custom-call | flops 10066329600 | bytes 24000000 | tf_op jit(solution)/shard_map/main_first/pallas_call | solution.py:145
  55.8 3.0 %weights.1 = (bf16[1024,256]{1,0:T(8,128)(2,1)}, f32[1,256]{1,0:T(1,128)}, bf16[1152,256]{1,0:T(8,128)(2,1)}, f32[1,256]{1,0:T(1,128)}, bf16[1536,256]{1,0:T(8,1...) custom-call(bf16[3,3,64,64]{3,2,1,0:T(8,128)(2,1)} %rw1_ref, f32[1,64]{1,0:T(1,128)} %bitcast.36, ...), custom_call_target="tpu_custom_call" | custom-call | flops 4000000 | bytes 5000000 | tf_op jit(solution)/shard_map/weights/pallas_call | solution.py:315
  58.9 0.7 copy-done.8
  59.8 8.0 %edge_first.1 = (bf16[73,7,16,256]{3,2,1,0:T(8,128)(2,1)}, bf16[73,2,16,256]{3,2,1,0:T(8,128)(2,1)}) custom-call(bf16[296,16,128]{2,1,0:T(8,128)(2,1)} %get-tuple-element.31.own0_ref, bf16[296,16,128]{2,1,0:T(8,128)(2,1)} %get-tuple-element.32.own5_ref, bf16[148,16,128]{2,1,0:T(8,128)(2,1)} %copy-done.7, bf16[74,16,128]{2,1,0:T(8,128)(2,1)} %copy-done.8, ...), custom_call_target="tpu_custom_call" | custom-call | flops 2831155200 | bytes 12000000 | tf_op jit(solution)/shard_map/edge_first/pallas_call | solution.py:199
  67.8 29.5 %shard_map.127 = bf16[73,36,16,256]{3,2,1,0:T(8,128)(2,1)} custom-call(bf16[73,7,16,256]{3,2,1,0:T(8,128)(2,1)} %get-tuple-element.36.refs_0_, bf16[73,28,16,256]{3,2,1,0:T(8,128)(2,1)} %get-tuple-element.37.refs_1_, bf16[73,2,16,256]{3,2,1,0:T(8,128)(2,1)} %get-tuple-element.38.refs_2_, bf16[1024,256]{1,0:T(8,128)(2,1)} %get-tuple-element.46.refs_3_, ...), custom_call_target="tpu_custom_call" | custom-call | flops 21743271936 | bytes 40000000 | tf_op jit(solution)/shard_map/pallas_call | solution.py:243
  97.3 20.3 %shard_map.128 = bf16[72,18,16,256]{3,2,1,0:T(8,128)(2,1)} custom-call(bf16[73,18,2,16,256]{4,3,2,1,0:T(8,128)(2,1)} %bitcast.45, bf16[1152,256]{1,0:T(8,128)(2,1)} %get-tuple-element.48.refs_1_, f32[1,256]{1,0:T(1,128)} %get-tuple-element.49.refs_2_), custom_call_target="tpu_custom_call" | custom-call | flops 12230590464 | bytes 40000000 | tf_op jit(solution)/shard_map/pallas_call | solution.py:243
  117.6 2.4 %fusion.27 = (bf16[72,3,16,256]{3,2,1,0:T(8,128)(2,1)S(1)}, bf16[72,3,16,256]{3,2,1,0:T(8,128)(2,1)S(1)}) fusion(bf16[72,18,16,256]{3,2,1,0:T(8,128)(2,1)} %shard_map.128), kind=kLoop, calls=%fused_computation.30 | loop fusion | bytes 7077888 | tf_op jit(solution)/shard_map/slice | solution.py:351
  120.1 4.0 %maximum_convert_fusion.3 = bf16[70,2,32,256]{3,2,1,0:T(8,128)(2,1)S(1)} fusion(f32[256]{0:T(256)S(1)} %bitcast.43, bf16[3,2,256,256]{3,2,1,0:T(8,128)(2,1)S(1)} %bitcast.41, bf16[72,3,16,256]{3,2,1,0:T(8,128)(2,1)S(1)} %get-tuple-element.58, bf16[72,3,16,256]{3,2,1,0:T(8,128)(2,1)S(1)} %get-tuple-element.57), kind=kOutput, calls=%fused_computation.15 | convolution fusion | flops 3533733888 | bytes 6620160 | tf_op jit(solution)/shard_map/conv_general_dilated | solution.py:324
  124.2 1.0 fusion.23
  125.3 3.9 %collective-permute-start.5 = (bf16[34,1,16,256]{3,2,1,0:T(8,128)(2,1)S(1)}, bf16[34,1,16,256]{3,2,1,0:T(8,128)(2,1)S(1)}, u32[]{:S(2)}, u32[]{:S(2)}) collective-permute-start(bf16[34,1,16,256]{3,2,1,0:T(8,128)(2,1)S(1)} %get-tuple-element.65), channel_id=1, source_target_pairs={{0,12},{4,0},{8,4},{12,8},{1,13},{5,1},{9,5},{13,9},{2,14},{6,2},{... | collective-permute-start | bytes 835592 | tf_op jit(solution)/shard_map/ppermute | solution.py:356
  129.2 12.4 %maximum_convert_fusion = bf16[70,13,16,256]{3,2,1,0:T(8,128)(2,1)S(1)} fusion(bf16[72,18,16,256]{3,2,1,0:T(8,128)(2,1)S(1)} %bitcast.31, bf16[3,2,256,256]{3,2,1,0:T(8,128)(2,1)S(1)} %bitcast.42, f32[256]{0:T(256)S(1)} %bitcast.44), kind=kOutput, calls=%fused_computation | convolution fusion | flops 11461632000 | bytes 18859008 | tf_op jit(solution)/shard_map/conv_general_dilated | solution.py:324
  141.7 7.5 %maximum_convert_fusion.2 = bf16[34,14,16,256]{3,2,1,0:T(8,128)(2,1)S(1)} fusion(f32[256]{0:T(256)S(1)} %copy-done.9, bf16[3,2,256,256]{3,2,1,0:T(8,128)(2,1)S(1)} %bitcast.40, bf16[70,1,16,256]{3,2,1,0:T(8,128)(2,1)S(1)} %get-tuple-element.62, bf16[70,13,16,256]{3,2,1,0:T(8,128)(2,1)S(1)} %maximum_convert_fusion, ...), kind=kOutput, calls=%fused_computation.8 | convolution fusion | flops 6003916800 | bytes 13288448 | tf_op jit(solution)/shard_map/conv_general_dilated | solution.py:324
  149.4 10.5 %maximum_convert_fusion.1 = bf16[32,16,16,256]{3,2,1,0:T(8,128)(2,1)S(1)} fusion(f32[256]{0:T(256)S(1)} %copy-done.10, bf16[3,3,256,256]{3,2,1,0:T(8,128)(2,1)S(1)} %copy-done, bf16[34,2,16,256]{3,2,1,0:T(8,128)(2,1)S(1)} %pad_maximum_fusion.1, bf16[34,14,16,256]{3,2,1,0:T(8,128)(2,1)S(1)} %maximum_convert_fusion.2, ...), kind=kOutput, calls=%fused_computation.7 | convolution fusion | flops 9674981376 | bytes 10388480 | tf_op jit(solution)/shard_map/conv_general_dilated | solution.py:324
  159.9 3.5 %copy.17 = bf16[16,32,16,256]{3,2,1,0:T(8,128)(2,1)} copy(bf16[16,32,16,256]{3,0,2,1:T(8,128)(2,1)S(1)} %bitcast.28) | data formatting | bytes 8388608 | tf_op jit(solution)/shard_map/transpose | solution.py:367
  (46 shorter events, 3.0 us)
Async XLA Ops:
  0.0 149.4 %copy-start = (bf16[3,3,256,256]{3,2,1,0:T(8,128)(2,1)S(1)}, bf16[3,3,256,256]{3,2,1,0:T(8,128)(2,1)}, u32[]{:S(2)}) copy-start(bf16[3,3,256,256]{3,2,1,0:T(8,128)(2,1)} %param.24) | copy-start | bytes 3538948
  0.0 12.4 %copy-start.4 = (f32[64]{0:T(128)S(1)}, f32[64]{0:T(128)}, u32[]{:S(2)}) copy-start(f32[64]{0:T(128)} %param.15) | copy-start | bytes 772
  0.0 13.1 %copy-start.3 = (bf16[3,3,4,64]{3,2,1,0:T(4,128)(2,1)S(1)}, bf16[3,3,4,64]{3,2,1,0:T(4,128)(2,1)}, u32[]{:S(2)}) copy-start(bf16[3,3,4,64]{3,2,1,0:T(4,128)(2,1)} %param.14) | copy-start | bytes 13828
  7.1 2.1 %copy-start.1 = (bf16[16,256,128,4]{2,0,3,1:T(8,128)(2,1)}, bf16[16,256,128,4]{2,0,3,1:T(8,128)(2,1)S(1)}, u32[]{:S(2)}) copy-start(bf16[16,256,128,4]{2,0,3,1:T(8,128)(2,1)S(1)} %copy.20) | copy-start | bytes 12582916
  8.0 10.8 %collective-permute-start = (bf16[16,24,4,128]{3,0,2,1:T(8,128)(2,1)}, bf16[16,24,4,128]{3,0,2,1:T(8,128)(2,1)}, u32[]{:S(2)}, u32[]{:S(2)}) collective-permute-start(bf16[16,24,4,128]{3,0,2,1:T(8,128)(2,1)} %slice.41), channel_id=1, source_target_pairs={{0,1},{1,2},{2,3},{3,0},{4,5},{5,6},{6,7},{7,4},{8,9},{9,10},{10,1... | collective-permute-start | bytes 1179656 | tf_op jit(solution)/shard_map/ppermute | solution.py:335
  10.0 8.9 %collective-permute-start.1 = (bf16[16,16,4,128]{3,0,2,1:T(8,128)(2,1)}, bf16[16,16,4,128]{3,0,2,1:T(8,128)(2,1)S(1)}, u32[]{:S(2)}, u32[]{:S(2)}) collective-permute-start(bf16[16,16,4,128]{3,0,2,1:T(8,128)(2,1)} %slice.42), channel_id=1, source_target_pairs={{0,3},{1,0},{2,1},{3,2},{4,7},{5,4},{6,5},{7,6},{8,11},{9,8},{10,9... | collective-permute-start | bytes 786440 | tf_op jit(solution)/shard_map/ppermute | solution.py:336
  18.9 0.7 copy-start.2
  25.9 32.9 %collective-permute-start.3 = (bf16[74,16,128]{2,1,0:T(8,128)(2,1)}, bf16[74,16,128]{2,1,0:T(8,128)(2,1)S(1)}, u32[]{:S(2)}, u32[]{:S(2)}) collective-permute-start(bf16[74,16,128]{2,1,0:T(8,128)(2,1)} %get-tuple-element.35), channel_id=1, source_target_pairs={{0,12},{4,0},{8,4},{12,8},{1,13},{5,1},{9,5},{13,9},{2,14},{6,2},{... | collective-permute-start | bytes 909320 | tf_op jit(solution)/shard_map/ppermute | solution.py:343
  29.5 29.3 %collective-permute-start.2 = (bf16[148,16,128]{2,1,0:T(8,128)(2,1)}, bf16[148,16,128]{2,1,0:T(8,128)(2,1)S(1)}, u32[]{:S(2)}, u32[]{:S(2)}) collective-permute-start(bf16[148,16,128]{2,1,0:T(8,128)(2,1)} %get-tuple-element.34), channel_id=1, source_target_pairs={{0,4},{4,8},{8,12},{12,0},{1,5},{5,9},{9,13},{13,1},{2,6},{6,10},{... | collective-permute-start | bytes 1818632 | tf_op jit(solution)/shard_map/ppermute | solution.py:342
  58.8 0.7 copy-start.8
  58.9 0.9 copy-start.7
  117.6 2.4 %copy-start.6 = (bf16[1536,256]{1,0:T(8,128)(2,1)S(1)}, bf16[1536,256]{1,0:T(8,128)(2,1)}, u32[]{:S(2)}) copy-start(bf16[1536,256]{1,0:T(8,128)(2,1)} %get-tuple-element.50) | copy-start | bytes 2359300
  117.6 2.4 %copy-start.11 = (f32[1,256]{1,0:T(1,128)S(1)}, f32[1,256]{1,0:T(1,128)}, u32[]{:S(2)}) copy-start(f32[1,256]{1,0:T(1,128)} %get-tuple-element.51) | copy-start | bytes 3076
  117.6 11.6 %slice-start = ((s8[10616832]{0:T(1024)(128)(4,1)}), s8[4194304]{0:T(1024)(128)(4,1)S(1)}, s32[]{:S(2)}) async-start(s8[10616832]{0:T(1024)(128)(4,1)} %bitcast.30), calls=%async_computation | async-start | bytes 8388608
  120.1 4.2 %copy-start.5 = (bf16[1536,256]{1,0:T(8,128)(2,1)S(1)}, bf16[1536,256]{1,0:T(8,128)(2,1)}, u32[]{:S(2)}) copy-start(bf16[1536,256]{1,0:T(8,128)(2,1)} %get-tuple-element.52) | copy-start | bytes 2359300
  120.1 4.2 %copy-start.9 = (f32[256]{0:T(256)S(1)}, f32[256]{0:T(256)}, u32[]{:S(2)}) copy-start(f32[256]{0:T(256)} %param.23) | copy-start | bytes 3076
  120.1 9.1 %slice-start.1 = ((s8[10616832]{0:T(1024)(128)(4,1)}), s8[4194304]{0:T(1024)(128)(4,1)S(1)}, s32[]{:S(2)}) async-start(s8[10616832]{0:T(1024)(128)(4,1)} %bitcast.30), calls=%async_computation.1 | async-start | bytes 8388608
  120.1 9.1 %slice-start.2 = ((s8[10616832]{0:T(1024)(128)(4,1)}), s8[2228224]{0:T(1024)(128)(4,1)S(1)}, s32[]{:S(2)}) async-start(s8[10616832]{0:T(1024)(128)(4,1)} %bitcast.30), calls=%async_computation.2 | async-start | bytes 4456448
  125.3 23.9 %collective-permute-start.5 = (bf16[34,1,16,256]{3,2,1,0:T(8,128)(2,1)S(1)}, bf16[34,1,16,256]{3,2,1,0:T(8,128)(2,1)S(1)}, u32[]{:S(2)}, u32[]{:S(2)}) collective-permute-start(bf16[34,1,16,256]{3,2,1,0:T(8,128)(2,1)S(1)} %get-tuple-element.65), channel_id=1, source_target_pairs={{0,12},{4,0},{8,4},{12,8},{1,13},{5,1},{9,5},{13,9},{2,14},{6,2},{... | collective-permute-start | bytes 835592 | tf_op jit(solution)/shard_map/ppermute | solution.py:356
  129.2 20.1 %collective-permute-start.4 = (bf16[34,1,16,256]{3,2,1,0:T(8,128)(2,1)S(1)}, bf16[34,1,16,256]{3,2,1,0:T(8,128)(2,1)S(1)}, u32[]{:S(2)}, u32[]{:S(2)}) collective-permute-start(bf16[34,1,16,256]{3,2,1,0:T(8,128)(2,1)S(1)} %get-tuple-element.66), channel_id=1, source_target_pairs={{0,4},{4,8},{8,12},{12,0},{1,5},{5,9},{9,13},{13,1},{2,6},{6,10},{... | collective-permute-start | bytes 835592 | tf_op jit(solution)/shard_map/ppermute | solution.py:355
  141.7 7.7 %copy-start.10 = (f32[256]{0:T(256)S(1)}, f32[256]{0:T(256)}, u32[]{:S(2)}) copy-start(f32[256]{0:T(256)} %param.25) | copy-start | bytes 3076
